TPU v7x, 32 devices: a whole 2x2x4 slice. The times are simulated.
32 devices in a mesh: groups: 2 (over y), seq: 4 (over z), heads: 2 (over x), cfg: 2 (over core).
Axes of the slice: x: 2, y: 2, z: 4, core: 2. Of those that a mesh axis runs over, the one named last changes fastest.
Arguments:
- video_tokens: bfloat16 [2, 8, 1152, 1024], P('cfg', ('groups', 'seq'), 'heads'), parts along dimension 1, may hold values from -6 to 6
- text_tokens: bfloat16 [2, 8, 1152, 128], P('cfg', ('groups', 'seq'), 'heads'), parts along dimension 1, may hold values from -6 to 6
- text_length: int32 [2, 8], P('cfg', ('groups', 'seq')), parts along dimension 1, may hold values from 1 to 128
- guide_numer: int32 [8], P(('groups', 'seq')), parts along dimension 0, may hold values from 2 to 8
- guide_denom: int32 [8], P(('groups', 'seq')), parts along dimension 0, may hold values from 4 to 8
- spatial_gain: bfloat16 [1152], replicated, may hold values from 0.25 to 1.75
- spatial_qkv: bfloat16 [3, 1152, 1152], P(None, 'heads'), may hold values from -0.11785113 to 0.11785113
- spatial_out: bfloat16 [1152, 1152], P('heads'), may hold values from -0.1875 to 0.1875
- temporal_gain: bfloat16 [1152], replicated, may hold values from 0.25 to 1.75
- temporal_qkv: bfloat16 [3, 1152, 1152], P(None, 'heads'), may hold values from -0.11785113 to 0.11785113
- temporal_out: bfloat16 [1152, 1152], P('heads'), may hold values from -0.1875 to 0.1875
Outputs:
- guided: bfloat16 [8, 1152, 1024], P(('groups', 'seq'), ('heads', 'cfg')), parts along dimension 0
There are 2 independent parts, one for each index of `groups`. A program takes and returns all parts, laid end to end along the dimension named above; an argument that names none is the same for every part. Nothing has to cross between parts.
Inputs may be any that keep to these rules, and one draw needn't show every extreme that they name: `text_length`: text tokens at or beyond a frame's length are padding.
All inputs are finite; a program needn't handle non-finite values.
Results may differ from a plain program's by a relative error of at most 0.009.
Values may be sent and summed in bfloat16 or wider, within the bound.
A program may use at most 64 MiB of HBM per device.

v0:
```python
import jax
import jax.numpy as jnp
from jax import lax
from jax.sharding import PartitionSpec as P

D = 1152
HEAD_DIM = 72
epsilon = 1e-06


def from_partner(shard, axis, stride):
    return lax.ppermute(shard, axis, [(i, i ^ 1 << stride) for i in range(lax.axis_size(axis))])


def softmax_along(scores, axis):
    top_score = jnp.max(scores, axis=axis, keepdims=True)
    expons = jnp.exp(scores - top_score)
    return (expons / jnp.sum(expons, axis=axis, keepdims=True)).astype(jnp.bfloat16)


def project_piece(piece, gain_vector, weights, parts):
    gain_piece = gain_vector.astype(jnp.float32)
    weight_piece = weights[parts]
    piece_wide = piece.astype(jnp.float32)
    scaled = (piece_wide * gain_piece[None, :, None]).astype(jnp.bfloat16)
    product = jnp.einsum("kod,fdp->fkop", weight_piece, scaled, preferred_element_type=jnp.float32)
    return (product, jnp.sum(piece_wide * piece_wide, axis=1))


def add_mixed(piece, matrix):
    return jnp.einsum("oc,fcp->fop", matrix, piece, preferred_element_type=jnp.float32)


def shards(
    video_tokens,
    text_tokens,
    text_length,
    guide_numer,
    guide_denom,
    spatial_gain,
    spatial_qkv,
    spatial_out,
    temporal_gain,
    temporal_qkv,
    temporal_out,
):
    frame_count = video_tokens.shape[1]
    width = video_tokens.shape[2]
    positions = video_tokens.shape[3]
    text_count = text_tokens.shape[3]
    local_heads = width // HEAD_DIM
    frame_tokens = video_tokens[0]
    frame_text = text_tokens[0]
    video_piece = lax.all_gather(frame_tokens, "heads", axis=1, tiled=True)
    text_piece = lax.all_gather(frame_text, "heads", axis=1, tiled=True)
    video_add, video_sq = project_piece(video_piece, spatial_gain, spatial_qkv, slice(0, 3))
    text_add, text_sq = project_piece(text_piece, spatial_gain, spatial_qkv, slice(1, 3))
    mixed = (video_add * lax.rsqrt(video_sq / D + epsilon)[:, None, None, :]).astype(jnp.bfloat16)
    mixed = mixed.reshape(frame_count, 3, local_heads, HEAD_DIM, positions)
    context = (text_add * lax.rsqrt(text_sq / D + epsilon)[:, None, None, :]).astype(jnp.bfloat16)
    context = context.reshape(frame_count, 2, local_heads, HEAD_DIM, text_count)
    key_rows = jnp.concatenate([mixed[:, 1], context[:, 0]], axis=3)
    value_rows = jnp.concatenate([mixed[:, 2], context[:, 1]], axis=3)
    query_all = mixed[:, 0]
    text_valid = jnp.arange(text_count, dtype=jnp.int32)[None, :] < text_length[0][:, None]
    valid_keys = jnp.concatenate(
        [jnp.ones((frame_count, positions), dtype=bool), text_valid], axis=1
    )
    block_rows = min(512, positions)
    block_count = positions // block_rows
    frame_ids = jnp.repeat(jnp.arange(frame_count, dtype=jnp.int32), block_count)
    block_ids = jnp.tile(jnp.arange(block_count, dtype=jnp.int32), frame_count)

    def block_step(inputs):
        frame_id, block_id = inputs
        query_rows = lax.dynamic_slice_in_dim(
            query_all[frame_id], block_id * block_rows, block_rows, 2
        )
        scores = jnp.einsum(
            "hep,hek->hpk", query_rows, key_rows[frame_id], preferred_element_type=jnp.float32
        )
        scores = scores * HEAD_DIM ** (-0.5)
        scores = jnp.where(valid_keys[frame_id][None, None, :], scores, -jnp.inf)
        weights = softmax_along(scores, 2)
        result = jnp.einsum(
            "hpk,hek->hep", weights, value_rows[frame_id], preferred_element_type=jnp.float32
        )
        return result.astype(jnp.bfloat16)

    attended = lax.map(block_step, (frame_ids, block_ids))
    attended = attended.reshape(frame_count, block_count, local_heads, HEAD_DIM, block_rows)
    attended = jnp.transpose(attended, (0, 2, 3, 1, 4)).reshape(frame_count, width, positions)
    update = add_mixed(lax.all_gather(attended, "heads", axis=1, tiled=True), spatial_out)
    after_spatial = (frame_tokens.astype(jnp.float32) + update).astype(jnp.bfloat16)
    own_rows = lax.all_to_all(after_spatial, "seq", split_axis=2, concat_axis=0, tiled=True)
    frames_all = own_rows.shape[0]
    columns = own_rows.shape[2]
    piece_add, piece_sq = project_piece(
        lax.all_gather(own_rows, "heads", axis=1, tiled=True),
        temporal_gain,
        temporal_qkv,
        slice(0, 3),
    )
    mixed_time = (piece_add * lax.rsqrt(piece_sq / D + epsilon)[:, None, None, :]).astype(
        jnp.bfloat16
    )
    mixed_time = mixed_time.reshape(frames_all, 3, local_heads, HEAD_DIM, columns)
    time_scores = jnp.einsum(
        "fhep,ghep->hfgp", mixed_time[:, 0], mixed_time[:, 1], preferred_element_type=jnp.float32
    )
    time_weights = softmax_along(time_scores * HEAD_DIM ** (-0.5), 2)
    attended_time = jnp.einsum(
        "hfgp,ghep->fhep", time_weights, mixed_time[:, 2], preferred_element_type=jnp.float32
    )
    attended_time = attended_time.astype(jnp.bfloat16).reshape(frames_all, width, columns)
    update_time = add_mixed(
        lax.all_gather(attended_time, "heads", axis=1, tiled=True), temporal_out
    )
    block_out = (own_rows.astype(jnp.float32) + update_time).astype(jnp.bfloat16)
    returned = lax.all_to_all(block_out, "seq", split_axis=0, concat_axis=2, tiled=True)
    half_width = width // 2
    partner = from_partner(returned, "cfg", 0)
    branch_index = lax.axis_index("cfg")
    cond_full = jnp.where(branch_index == 0, returned, partner)
    uncond_full = jnp.where(branch_index == 0, partner, returned)
    cond_part = lax.dynamic_slice_in_dim(cond_full, branch_index * half_width, half_width, 1)
    uncond_part = lax.dynamic_slice_in_dim(uncond_full, branch_index * half_width, half_width, 1)
    ratio = guide_numer.astype(jnp.float32) / guide_denom.astype(jnp.float32)
    cond_wide = cond_part.astype(jnp.float32)
    uncond_wide = uncond_part.astype(jnp.float32)
    return (uncond_wide + ratio[:, None, None] * (cond_wide - uncond_wide)).astype(jnp.bfloat16)


def solution(mesh):
    return jax.shard_map(
        shards,
        mesh=mesh,
        in_specs=(
            P("cfg", ("groups", "seq"), "heads", None),
            P("cfg", ("groups", "seq"), "heads", None),
            P("cfg", ("groups", "seq")),
            P(("groups", "seq")),
            P(("groups", "seq")),
            P(),
            P(None, "heads", None),
            P("heads", None),
            P(),
            P(None, "heads", None),
            P("heads", None),
        ),
        out_specs=P(("groups", "seq"), ("heads", "cfg"), None),
        check_vma=False,
    )
```

profile of v0, /device:TPU:0, one launch (start us, length us, event | category | flops | bytes accessed | tf_op | source)
XLA Modules:
  0.0 359.0 jit_solution(843548291912899709)
XLA Ops:
  8.7 7.7 %all-gather.1 = bf16[1,1,1152,128]{3,2,1,0:T(8,128)(2,1)S(1)} all-gather(bf16[1,1,576,128]{3,2,1,0:T(8,128)(2,1)} %param.14), channel_id=3, replica_groups=mesh['groups'=2,'seq'=4,'heads'=2,'cfg'=2] {'heads'}, dimensions={2}, use_global_device_ids=true | all-gather | bytes 442368 | tf_op jit(solution)/shard_map/all_gather | solution.py:55
  16.6 3.0 fusion.87
  19.6 28.1 %all-gather.12.cloned.1.call-done = bf16[1,1,1152,1024]{3,2,1,0:T(8,128)(2,1)} async-done(((bf16[1,1,576,1024]{3,2,1,0:T(8,128)(2,1)}), bf16[1,1,1152,1024]{3,2,1,0:T(8,128)(2,1)}) %all-gather.12.cloned.1.call-update) | async-done | bytes 2359312 | tf_op jit(solution)/shard_map/all_gather | solution.py:54
  47.7 2.3 fusion.50
  50.1 7.3 %fusion.48 = bf16[1,1024,3,576]{1,3,2,0:T(8,128)(2,1)S(1)} fusion(f32[1024]{0:T(1024)S(1)} %add_rsqrt_fusion.1, bf16[3,576,1152]{2,1,0:T(8,128)(2,1)} %param.19, bf16[1,1,1152,1024]{3,2,1,0:T(8,128)(2,1)S(1)} %copy-done.3, f32[1152]{0:T(1024)S(1)} %convert_element_type.98), kind=kOutput, calls=%fused_computation.28 | convolution fusion | flops 4083941376 | bytes 9888256 | tf_op jit(solution)/shard_map/kod,fdp->fkop/dot_general | solution.py:26
  60.1 37.0 %while.10 = (s32[]{:T(128)}, bf16[2,8,72,512]{3,2,1,0:T(8,128)(2,1)}, pred[1,1152]{1,0:T(4,128)(4,1)S(1)}, s32[2]{0:T(128)S(1)}, bf16[1,8,72,1024]{3,2,1,0:T(8,1...) while((s32[]{:T(128)}, ...), condition=%wide.region_5.6_spmd, body=%wide.region_2.5_spmd.sunk | while | flops 2081200384 | bytes 5788856 | solution.py:90
  61.9 7.0 %exponential_reduce_fusion.2 = f32[8,512]{1,0:T(8,128)S(1)} fusion(pred[1152]{0:T(1024)(128)(4,1)S(1)} %reduce.5, bf16[1,8,72,1152]{3,2,1,0:T(8,128)(2,1)S(1)} %get-tuple-element.139, bf16[1,8,72,1024]{3,2,1,0:T(8,128)(2,1)} %get-tuple-element.138, s32[]{:T(128)S(6)} %select_n.52), kind=kOutput, calls=%fused_computation.5.clone.1 | convolution fusion | flops 698352768 | bytes 1934468 | tf_op jit(solution)/shard_map/while/body/eval_jaxpr/sub | solution.py:17
  69.0 9.8 %fusion.120 = bf16[2,8,72,512]{3,2,1,0:T(8,128)(2,1)} fusion(bf16[2,8,72,512]{3,2,1,0:T(8,128)(2,1)} %get-tuple-element.123, s32[]{:T(128)} %get-tuple-element.122, bf16[1,8,72,1152]{3,2,1,0:T(8,128)(2,1)} %get-tuple-element.140, f32[8,512]{1,0:T(8,128)S(1)} %exponential_reduce_fusion.2, pred[1152]{0:T(1024)(128)(4,1)S(1)} %reduce.5, ...), kind=kOutput, calls=%fused_computation.13.clone.1 | convolution fusion | flops 1382847616 | bytes 3851908 | tf_op jit(solution)/shard_map/while/body/eval_jaxpr/hpk,hek->hep/dot_general | solution.py:85
  80.2 7.0 %exponential_reduce_fusion.2 = f32[8,512]{1,0:T(8,128)S(1)} fusion(pred[1152]{0:T(1024)(128)(4,1)S(1)} %reduce.5, bf16[1,8,72,1152]{3,2,1,0:T(8,128)(2,1)S(1)} %get-tuple-element.139, bf16[1,8,72,1024]{3,2,1,0:T(8,128)(2,1)} %get-tuple-element.138, s32[]{:T(128)S(6)} %select_n.52), kind=kOutput, calls=%fused_computation.5.clone.1 | convolution fusion | flops 698352768 | bytes 1934468 | tf_op jit(solution)/shard_map/while/body/eval_jaxpr/sub | solution.py:17
  87.2 9.8 %fusion.120 = bf16[2,8,72,512]{3,2,1,0:T(8,128)(2,1)} fusion(bf16[2,8,72,512]{3,2,1,0:T(8,128)(2,1)} %get-tuple-element.123, s32[]{:T(128)} %get-tuple-element.122, bf16[1,8,72,1152]{3,2,1,0:T(8,128)(2,1)} %get-tuple-element.140, f32[8,512]{1,0:T(8,128)S(1)} %exponential_reduce_fusion.2, pred[1152]{0:T(1024)(128)(4,1)S(1)} %reduce.5, ...), kind=kOutput, calls=%fused_computation.13.clone.1 | convolution fusion | flops 1382847616 | bytes 3851908 | tf_op jit(solution)/shard_map/while/body/eval_jaxpr/hpk,hek->hep/dot_general | solution.py:85
  97.1 2.5 copy.43
  101.5 36.0 %all-gather.8.cloned.1.call-done = bf16[1,1152,1024]{2,1,0:T(8,128)(2,1)} async-done(((bf16[1,576,1024]{2,1,0:T(8,128)(2,1)}), bf16[1,1152,1024]{2,1,0:T(8,128)(2,1)}) %all-gather.8.cloned.1.call-update) | async-done | bytes 2359312 | tf_op jit(solution)/shard_map/all_gather | solution.py:93
  137.5 3.7 %fusion.64 = bf16[1,576,1024]{2,1,0:T(8,128)(2,1)S(1)} fusion(bf16[576,1152]{1,0:T(8,128)(2,1)S(1)} %copy-done, bf16[1,1152,1024]{2,1,0:T(8,128)(2,1)} %all-gather.8.cloned.1.call-done, bf16[1,1,576,1024]{3,2,1,0:T(8,128)(2,1)} %param.13), kind=kOutput, calls=%fused_computation.47 | convolution fusion | flops 1360723968 | bytes 6045696 | tf_op jit(solution)/shard_map/oc,fcp->fop/dot_general | solution.py:31
  141.1 4.1 %copy.44 = bf16[1,576,1024]{1,0,2:T(2,128)(2,1)} copy(bf16[1,576,1024]{2,1,0:T(8,128)(2,1)S(1)} %fusion.64) | data formatting | bytes 2359296 | tf_op jit(solution)/shard_map/convert_element_type | solution.py:94
  145.8 9.9 %reduce.3 = bf16[1024,576]{1,0:T(8,128)(2,1)S(1)} reduce(bf16[1024,1,576]{2,1,0:T(2,128)(2,1)} %bitcast.189, bf16[]{:T(256)} %broadcast.82), dimensions={1}, to_apply=%bitcast.164.reduce_sub_computation | reduce | bytes 2359298
  155.7 2.6 reshape.124
  158.3 33.0 %all_to_all.36 = bf16[4,2,73728]{2,1,0:T(2,128)(2,1)S(1)} all-to-all(bf16[4,2,73728]{2,1,0:T(2,128)(2,1)} %reshape.124), channel_id=1, replica_groups=mesh['groups'=2,'seq'=4,'heads'=2,'cfg'=2] {'seq'}, dimensions={0} | all-to-all | bytes 2359296 | tf_op jit(solution)/shard_map/all_to_all | solution.py:95
  191.3 3.3 reshape.125
  198.3 34.1 %all-gather.14.cloned.1.call-done = bf16[4,1,1152,256]{3,2,0,1:T(8,128)(2,1)} async-done(((bf16[4,1,576,256]{3,2,0,1:T(8,128)(2,1)}), bf16[4,1,1152,256]{3,2,0,1:T(8,128)(2,1)}) %all-gather.14.cloned.1.call-update) | async-done | bytes 2359312 | tf_op jit(solution)/shard_map/all_gather | solution.py:99
  232.3 2.3 fusion.52
  234.7 7.2 %multiply_convert_fusion = bf16[4,256,3,576]{1,3,2,0:T(8,128)(2,1)S(1)} fusion(f32[4,256]{1,0:T(4,128)S(1)} %add_rsqrt_fusion, bf16[3,576,1152]{2,1,0:T(8,128)(2,1)} %param.22, bf16[4,1,1152,256]{3,2,0,1:T(8,128)(2,1)S(1)} %copy-done.4, f32[1152]{0:T(1024)S(1)} %convert_element_type.109), kind=kOutput, calls=%fused_computation.29 | convolution fusion | flops 4083941376 | bytes 9888256 | tf_op jit(solution)/shard_map/kod,fdp->fkop/dot_general | solution.py:26
  243.8 2.8 copy.59
  246.7 4.1 %copy.60 = bf16[4,1,8,72,256]{3,0,4,2,1:T(4,128)(2,1)} copy(bf16[4,1,8,72,256]{4,3,2,1,0:T(8,128)(2,1)} %get-tuple-element.59) | data formatting | bytes 2359296
  250.7 5.8 %fusion.71 = f32[8,256,4,4]{3,2,1,0:T(4,128)} fusion(bf16[4,1,8,72,256]{3,0,4,2,1:T(4,128)(2,1)} %copy.60, bf16[4,1,8,72,256]{3,0,4,2,1:T(4,128)(2,1)S(1)} %copy.59), kind=kOutput, calls=%fused_computation.54 | convolution fusion | flops 4718592 | bytes 2490368 | tf_op jit(solution)/shard_map/fhep,ghep->hfgp/dot_general | solution.py:108
  256.5 2.8 copy.50
  261.6 2.5 copy.58
  264.1 5.8 %convert_bitcast_fusion = bf16[4,8,72,256]{2,0,3,1:T(4,128)(2,1)} fusion(bf16[8,4,4,256]{2,1,3,0:T(4,128)(2,1)} %copy.51, bf16[4,1,8,72,256]{3,0,4,2,1:T(4,128)(2,1)} %copy.58), kind=kOutput, calls=%fused_computation.59 | convolution fusion | flops 5308416 | bytes 2424832 | tf_op jit(solution)/shard_map/hfgp,ghep->fhep/dot_general | solution.py:112
  269.9 4.2 %copy.52 = bf16[4,8,72,256]{3,2,1,0:T(8,128)(2,1)} copy(bf16[4,8,72,256]{2,0,3,1:T(4,128)(2,1)} %convert_bitcast_fusion) | data formatting | bytes 2359296 | tf_op jit(solution)/shard_map/convert_element_type | solution.py:115
  274.1 36.2 %all-gather.10.cloned.1.call-done = bf16[4,1152,256]{2,1,0:T(8,128)(2,1)} async-done(((bf16[4,576,256]{2,1,0:T(8,128)(2,1)}), bf16[4,1152,256]{2,1,0:T(8,128)(2,1)}) %all-gather.10.cloned.1.call-update) | async-done | bytes 2359312 | tf_op jit(solution)/shard_map/all_gather | solution.py:117
  310.3 3.8 %fusion.63 = bf16[4,576,256]{2,1,0:T(8,128)(2,1)S(1)} fusion(bf16[4,1152,256]{2,1,0:T(8,128)(2,1)} %all-gather.10.cloned.1.call-done, bf16[576,1152]{1,0:T(8,128)(2,1)} %param.23, bf16[1,576,4,256]{3,1,2,0:T(8,128)(2,1)S(1)} %copy-done.2), kind=kOutput, calls=%fused_computation.45 | convolution fusion | flops 1360723968 | bytes 6045696 | tf_op jit(solution)/shard_map/oc,fcp->fop/dot_general | solution.py:31
  314.1 32.8 %all_to_all.37 = bf16[4,576,256]{2,1,0:T(8,128)(2,1)S(1)} all-to-all(bf16[4,576,256]{2,1,0:T(8,128)(2,1)S(1)} %fusion.63), channel_id=1, replica_groups=mesh['groups'=2,'seq'=4,'heads'=2,'cfg'=2] {'seq'}, dimensions={0} | all-to-all | bytes 2359296 | tf_op jit(solution)/shard_map/all_to_all | solution.py:120
  350.0 2.2 fusion.91
  (49 shorter events, 17.9 us)
Async XLA Ops:
  6.5 130.9 %copy-start = (bf16[576,1152]{1,0:T(8,128)(2,1)S(1)}, bf16[576,1152]{1,0:T(8,128)(2,1)}, u32[]{:S(2)}) copy-start(bf16[576,1152]{1,0:T(8,128)(2,1)} %param.20) | copy-start | bytes 3981316
  6.5 41.1 %all-gather.12.cloned.1.call-start = ((), (), s32[]{:S(2)}) async-start(), calls=%async_computation.4 | async-start | bytes 3538944 | tf_op jit(solution)/shard_map/all_gather | solution.py:54
  7.3 130.2 %all-gather.8.cloned.1.call-start = ((), (), s32[]{:S(2)}) async-start(), calls=%async_computation.2 | async-start | bytes 3538944 | tf_op jit(solution)/shard_map/all_gather | solution.py:93
  47.7 2.4 copy-start.3
  101.3 131.0 %all-gather.14.cloned.1.call-start = ((), (), s32[]{:S(2)}) async-start(), calls=%async_computation.5 | async-start | bytes 3538944 | tf_op jit(solution)/shard_map/all_gather | solution.py:99
  196.5 1.8 copy-start.5
  198.0 112.3 %all-gather.10.cloned.1.call-start = ((), (), s32[]{:S(2)}) async-start(), calls=%async_computation.3 | async-start | bytes 3538944 | tf_op jit(solution)/shard_map/all_gather | solution.py:117
  232.3 2.4 copy-start.4
  259.4 2.2 copy-start.1
  269.9 40.4 %copy-start.2 = (bf16[1,576,4,256]{3,1,2,0:T(8,128)(2,1)S(1)}, bf16[1,576,4,256]{3,1,2,0:T(8,128)(2,1)}, u32[]{:S(2)}) copy-start(bf16[1,576,4,256]{3,1,2,0:T(8,128)(2,1)} %copy.46) | copy-start | bytes 3538948
  347.0 3.0 collective-permute-start
Sparse Core Ops, SparseCore 0:
  8.9 38.7 all-gather.11
  101.4 36.0 all-gather.7
  198.1 34.1 all-gather.13
  274.2 36.0 all-gather.9
where the time goes:
time: 364 us; the launch traced here: 359 us
  waiting for transfers between devices  137 us (38%)
  blocking collectives  73.5 us (20%)
  matrix products  70.3 us (19%)
  local copies, waits for them, and re-layouts  41.4 us (11%)
  other arithmetic  19.1 us (5%)
  between operations  15.5 us (4%)
    all_gather x1, waiting for transfers between devices, shards(): lax.all_gather(attended_time, 'heads', axis=1, tiled=True)  36.2 us
    all_gather x1, waiting for transfers between devices, shards(): lax.all_gather(attended, 'heads', axis=1, tiled=True)  36 us
    all_gather x1, waiting for transfers between devices, shards(): lax.all_gather(own_rows, 'heads', axis=1, tiled=True)  34.1 us
    all_to_all x1, blocking collectives, shards(): lax.all_to_all(after_spatial, 'seq', split_axis=2, concat_axis=0, tiled=T...  33 us
    all_to_all x1, blocking collectives, shards(): lax.all_to_all(block_out, 'seq', split_axis=0, concat_axis=2, tiled=True)  32.8 us
    all_gather x1, waiting for transfers between devices, shards(): video_piece = lax.all_gather(frame_tokens, 'heads', axis=1, tiled=True)  28.1 us
    dot_general x2, matrix products, block_step(): jnp.einsum('hpk,hek->hep', weights, value_rows[frame_id], preferred_eleme...  19.7 us
    unnamed x19, local copies, waits for them, and re-layouts  17.8 us
  transfers between devices with their start and end apart: 5, of which 5 were waited for; matrix products, arithmetic and copies ran while one was open for 1% of the time, Pallas kernels for 0%

commit v1 on v0

--- a/solution.py
+++ b/solution.py
@@ -2,10 +2,26 @@
 import jax.numpy as jnp
 from jax import lax
 from jax.sharding import PartitionSpec as P
+from jax.lax import axis_index, axis_size, ppermute
 
 D = 1152
 HEAD_DIM = 72
 epsilon = 1e-06
+
+
+def draft_halves(local, axis_k, xx):
+    back = local.shape
+    return jnp.moveaxis(
+        local.reshape(*back[:axis_k], xx, back[axis_k] // xx, *back[axis_k + 1 :]), axis_k, 0
+    )
+
+
+def raise_pairs_all(field_in, which_dim):
+    field_in = jnp.moveaxis(field_in, 0, which_dim)
+    new = field_in.shape
+    return field_in.reshape(
+        *new[:which_dim], new[which_dim] * new[which_dim + 1], *new[which_dim + 2 :]
+    )
 
 
 def from_partner(shard, axis, stride):
@@ -117,7 +133,15 @@
         lax.all_gather(attended_time, "heads", axis=1, tiled=True), temporal_out
     )
     block_out = (own_rows.astype(jnp.float32) + update_time).astype(jnp.bfloat16)
-    returned = lax.all_to_all(block_out, "seq", split_axis=0, concat_axis=2, tiled=True)
+    main, frame_out = (axis_size("seq"), axis_index("seq"))
+    work_now = draft_halves(block_out, 0, main)
+    spare = work_now
+    for ii in range(1, main):
+        small, extra = ((frame_out + ii) % main, (frame_out - ii) % main)
+        v_next = lax.dynamic_index_in_dim(work_now, small, 0)
+        prior = ppermute(v_next, "seq", tuple(((t, (t + ii) % main) for t in range(main))))
+        spare = lax.dynamic_update_slice_in_dim(spare, prior, extra, axis=0)
+    returned = raise_pairs_all(spare, 2)
     half_width = width // 2
     partner = from_partner(returned, "cfg", 0)
     branch_index = lax.axis_index("cfg")

time: 364 us -> 361 us (level)
  the two profiles are of different devices: /device:TPU:0 before, /device:TPU:9 now
where the time goes in v1:
time: 361 us; the launch traced here: 357 us
  waiting for transfers between devices  163 us (45%)
  matrix products  70.1 us (19%)
  local copies, waits for them, and re-layouts  45.9 us (13%)
  blocking collectives  35.9 us (10%)
  other arithmetic  19.1 us (5%)
  between operations  15.6 us (4%)
  starting transfers between devices  4.71 us (1%)
    all_gather x1, waiting for transfers between devices, shards(): lax.all_gather(own_rows, 'heads', axis=1, tiled=True)  36.8 us
    all_gather x1, waiting for transfers between devices, shards(): lax.all_gather(attended_time, 'heads', axis=1, tiled=True)  36.2 us
    all_gather x1, waiting for transfers between devices, shards(): lax.all_gather(attended, 'heads', axis=1, tiled=True)  36 us
    all_to_all x1, blocking collectives, shards(): lax.all_to_all(after_spatial, 'seq', split_axis=2, concat_axis=0, tiled=T...  30.3 us
    all_gather x1, waiting for transfers between devices, shards(): video_piece = lax.all_gather(frame_tokens, 'heads', axis=1, tiled=True)  28.7 us
    ppermute x3, waiting for transfers between devices, shards(): ppermute(v_next, 'seq', tuple(((t, (t + ii) % main) for t in range(main))))  23.8 us
    dot_general x2, matrix products, block_step(): jnp.einsum('hpk,hek->hep', weights, value_rows[frame_id], preferred_eleme...  19.7 us
    unnamed x21, local copies, waits for them, and re-layouts  18.8 us
  transfers between devices with their start and end apart: 8, of which 8 were waited for; matrix products, arithmetic and copies ran while one was open for 1% of the time, Pallas kernels for 0%

profile of v1, /device:TPU:9, one launch (start us, length us, event | category | flops | bytes accessed | tf_op | source)
XLA Modules:
  0.0 356.5 jit_solution(16234193628592837940)
XLA Ops:
  8.7 5.6 %all-gather.1 = bf16[1,1,1152,128]{3,2,1,0:T(8,128)(2,1)S(1)} all-gather(bf16[1,1,576,128]{3,2,1,0:T(8,128)(2,1)} %param.14), channel_id=3, replica_groups=mesh['groups'=2,'seq'=4,'heads'=2,'cfg'=2] {'heads'}, dimensions={2}, use_global_device_ids=true | all-gather | bytes 442368 | tf_op jit(solution)/shard_map/all_gather | solution.py:71
  14.5 2.7 fusion.87
  17.2 28.7 %all-gather.12.cloned.1.call-done = bf16[1,1,1152,1024]{3,2,1,0:T(8,128)(2,1)} async-done(((bf16[1,1,576,1024]{3,2,1,0:T(8,128)(2,1)}), bf16[1,1,1152,1024]{3,2,1,0:T(8,128)(2,1)}) %all-gather.12.cloned.1.call-update) | async-done | bytes 2359312 | tf_op jit(solution)/shard_map/all_gather | solution.py:70
  45.9 2.3 fusion.50
  48.3 7.3 %fusion.48 = bf16[1,1024,3,576]{1,3,2,0:T(8,128)(2,1)S(1)} fusion(f32[1024]{0:T(1024)S(1)} %add_rsqrt_fusion.1, bf16[3,576,1152]{2,1,0:T(8,128)(2,1)} %param.19, bf16[1,1,1152,1024]{3,2,1,0:T(8,128)(2,1)S(1)} %copy-done.4, f32[1152]{0:T(1024)S(1)} %convert_element_type.98), kind=kOutput, calls=%fused_computation.28 | convolution fusion | flops 4083941376 | bytes 9888256 | tf_op jit(solution)/shard_map/kod,fdp->fkop/dot_general | solution.py:42
  58.3 37.0 %while.10 = (s32[]{:T(128)}, bf16[2,8,72,512]{3,2,1,0:T(8,128)(2,1)}, pred[1,1152]{1,0:T(4,128)(4,1)S(1)}, s32[2]{0:T(128)S(1)}, bf16[1,8,72,1024]{3,2,1,0:T(8,1...) while((s32[]{:T(128)}, ...), condition=%wide.region_5.6_spmd, body=%wide.region_2.5_spmd.sunk | while | flops 2081200384 | bytes 5788856 | solution.py:106
  60.2 7.0 %exponential_reduce_fusion.2 = f32[8,512]{1,0:T(8,128)S(1)} fusion(pred[1152]{0:T(1024)(128)(4,1)S(1)} %reduce.5, bf16[1,8,72,1152]{3,2,1,0:T(8,128)(2,1)S(1)} %get-tuple-element.142, bf16[1,8,72,1024]{3,2,1,0:T(8,128)(2,1)} %get-tuple-element.141, s32[]{:T(128)S(6)} %select_n.110), kind=kOutput, calls=%fused_computation.5.clone.1 | convolution fusion | flops 698352768 | bytes 1934468 | tf_op jit(solution)/shard_map/while/body/eval_jaxpr/sub | solution.py:33
  67.2 9.8 %fusion.120 = bf16[2,8,72,512]{3,2,1,0:T(8,128)(2,1)} fusion(bf16[2,8,72,512]{3,2,1,0:T(8,128)(2,1)} %get-tuple-element.126, s32[]{:T(128)} %get-tuple-element.125, bf16[1,8,72,1152]{3,2,1,0:T(8,128)(2,1)} %get-tuple-element.143, f32[8,512]{1,0:T(8,128)S(1)} %exponential_reduce_fusion.2, pred[1152]{0:T(1024)(128)(4,1)S(1)} %reduce.5, ...), kind=kOutput, calls=%fused_computation.13.clone.1 | convolution fusion | flops 1382847616 | bytes 3851908 | tf_op jit(solution)/shard_map/while/body/eval_jaxpr/hpk,hek->hep/dot_general | solution.py:101
  78.5 7.0 %exponential_reduce_fusion.2 = f32[8,512]{1,0:T(8,128)S(1)} fusion(pred[1152]{0:T(1024)(128)(4,1)S(1)} %reduce.5, bf16[1,8,72,1152]{3,2,1,0:T(8,128)(2,1)S(1)} %get-tuple-element.142, bf16[1,8,72,1024]{3,2,1,0:T(8,128)(2,1)} %get-tuple-element.141, s32[]{:T(128)S(6)} %select_n.110), kind=kOutput, calls=%fused_computation.5.clone.1 | convolution fusion | flops 698352768 | bytes 1934468 | tf_op jit(solution)/shard_map/while/body/eval_jaxpr/sub | solution.py:33
  85.5 9.8 %fusion.120 = bf16[2,8,72,512]{3,2,1,0:T(8,128)(2,1)} fusion(bf16[2,8,72,512]{3,2,1,0:T(8,128)(2,1)} %get-tuple-element.126, s32[]{:T(128)} %get-tuple-element.125, bf16[1,8,72,1152]{3,2,1,0:T(8,128)(2,1)} %get-tuple-element.143, f32[8,512]{1,0:T(8,128)S(1)} %exponential_reduce_fusion.2, pred[1152]{0:T(1024)(128)(4,1)S(1)} %reduce.5, ...), kind=kOutput, calls=%fused_computation.13.clone.1 | convolution fusion | flops 1382847616 | bytes 3851908 | tf_op jit(solution)/shard_map/while/body/eval_jaxpr/hpk,hek->hep/dot_general | solution.py:101
  95.4 2.5 copy.43
  99.8 36.0 %all-gather.8.cloned.1.call-done = bf16[1,1152,1024]{2,1,0:T(8,128)(2,1)} async-done(((bf16[1,576,1024]{2,1,0:T(8,128)(2,1)}), bf16[1,1152,1024]{2,1,0:T(8,128)(2,1)}) %all-gather.8.cloned.1.call-update) | async-done | bytes 2359312 | tf_op jit(solution)/shard_map/all_gather | solution.py:109
  135.7 3.7 %fusion.64 = bf16[1,576,1024]{2,1,0:T(8,128)(2,1)S(1)} fusion(bf16[576,1152]{1,0:T(8,128)(2,1)S(1)} %copy-done, bf16[1,1152,1024]{2,1,0:T(8,128)(2,1)} %all-gather.8.cloned.1.call-done, bf16[1,1,576,1024]{3,2,1,0:T(8,128)(2,1)} %param.13), kind=kOutput, calls=%fused_computation.47 | convolution fusion | flops 1360723968 | bytes 6045696 | tf_op jit(solution)/shard_map/oc,fcp->fop/dot_general | solution.py:47
  139.4 4.1 %copy.44 = bf16[1,576,1024]{1,0,2:T(2,128)(2,1)} copy(bf16[1,576,1024]{2,1,0:T(8,128)(2,1)S(1)} %fusion.64) | data formatting | bytes 2359296 | tf_op jit(solution)/shard_map/convert_element_type | solution.py:110
  144.0 9.9 %reduce.3 = bf16[1024,576]{1,0:T(8,128)(2,1)S(1)} reduce(bf16[1024,1,576]{2,1,0:T(2,128)(2,1)} %bitcast.194, bf16[]{:T(256)} %broadcast.88), dimensions={1}, to_apply=%bitcast.169.reduce_sub_computation | reduce | bytes 2359298
  154.0 2.6 reshape.135
  156.6 30.3 %all_to_all.18 = bf16[4,2,73728]{2,1,0:T(2,128)(2,1)S(1)} all-to-all(bf16[4,2,73728]{2,1,0:T(2,128)(2,1)} %reshape.135), channel_id=1, replica_groups=mesh['groups'=2,'seq'=4,'heads'=2,'cfg'=2] {'seq'}, dimensions={0} | all-to-all | bytes 2359296 | tf_op jit(solution)/shard_map/all_to_all | solution.py:111
  186.8 3.3 reshape.136
  193.8 36.8 %all-gather.14.cloned.1.call-done = bf16[4,1,1152,256]{3,2,0,1:T(8,128)(2,1)} async-done(((bf16[4,1,576,256]{3,2,0,1:T(8,128)(2,1)}), bf16[4,1,1152,256]{3,2,0,1:T(8,128)(2,1)}) %all-gather.14.cloned.1.call-update) | async-done | bytes 2359312 | tf_op jit(solution)/shard_map/all_gather | solution.py:115
  232.9 7.2 %multiply_convert_fusion = bf16[4,256,3,576]{1,3,2,0:T(8,128)(2,1)S(1)} fusion(f32[4,256]{1,0:T(4,128)S(1)} %add_rsqrt_fusion, bf16[3,576,1152]{2,1,0:T(8,128)(2,1)} %param.22, bf16[4,1,1152,256]{3,2,0,1:T(8,128)(2,1)S(1)} %copy-done.5, f32[1152]{0:T(1024)S(1)} %convert_element_type.109), kind=kOutput, calls=%fused_computation.29 | convolution fusion | flops 4083941376 | bytes 9888256 | tf_op jit(solution)/shard_map/kod,fdp->fkop/dot_general | solution.py:42
  242.1 2.8 copy.59
  244.9 4.1 %copy.60 = bf16[4,1,8,72,256]{3,0,4,2,1:T(4,128)(2,1)} copy(bf16[4,1,8,72,256]{4,3,2,1,0:T(8,128)(2,1)} %get-tuple-element.59) | data formatting | bytes 2359296
  249.0 5.8 %fusion.71 = f32[8,256,4,4]{3,2,1,0:T(4,128)} fusion(bf16[4,1,8,72,256]{3,0,4,2,1:T(4,128)(2,1)} %copy.60, bf16[4,1,8,72,256]{3,0,4,2,1:T(4,128)(2,1)S(1)} %copy.59), kind=kOutput, calls=%fused_computation.54 | convolution fusion | flops 4718592 | bytes 2490368 | tf_op jit(solution)/shard_map/fhep,ghep->hfgp/dot_general | solution.py:124
  254.8 2.8 copy.50
  259.9 2.5 copy.58
  262.3 5.8 %convert_bitcast_fusion = bf16[4,8,72,256]{2,0,3,1:T(4,128)(2,1)} fusion(bf16[8,4,4,256]{2,1,3,0:T(4,128)(2,1)} %copy.51, bf16[4,1,8,72,256]{3,0,4,2,1:T(4,128)(2,1)} %copy.58), kind=kOutput, calls=%fused_computation.59 | convolution fusion | flops 5308416 | bytes 2424832 | tf_op jit(solution)/shard_map/hfgp,ghep->fhep/dot_general | solution.py:128
  268.2 4.2 %copy.52 = bf16[4,8,72,256]{3,2,1,0:T(8,128)(2,1)} copy(bf16[4,8,72,256]{2,0,3,1:T(4,128)(2,1)} %convert_bitcast_fusion) | data formatting | bytes 2359296 | tf_op jit(solution)/shard_map/convert_element_type | solution.py:131
  272.4 36.2 %all-gather.10.cloned.1.call-done = bf16[4,1152,256]{2,1,0:T(8,128)(2,1)} async-done(((bf16[4,576,256]{2,1,0:T(8,128)(2,1)}), bf16[4,1152,256]{2,1,0:T(8,128)(2,1)}) %all-gather.10.cloned.1.call-update) | async-done | bytes 2359312 | tf_op jit(solution)/shard_map/all_gather | solution.py:133
  308.6 3.8 %fusion.63 = bf16[4,576,256]{2,1,0:T(8,128)(2,1)S(1)} fusion(bf16[4,1152,256]{2,1,0:T(8,128)(2,1)} %all-gather.10.cloned.1.call-done, bf16[576,1152]{1,0:T(8,128)(2,1)} %param.23, bf16[1,576,4,256]{3,1,2,0:T(8,128)(2,1)S(1)} %copy-done.2), kind=kOutput, calls=%fused_computation.45 | convolution fusion | flops 1360723968 | bytes 6045696 | tf_op jit(solution)/shard_map/oc,fcp->fop/dot_general | solution.py:47
  317.1 4.1 %collective-permute-done = bf16[1,1,576,256]{3,2,0,1:T(8,128)(2,1)S(1)} collective-permute-done((bf16[1,1,576,256]{3,2,0,1:T(8,128)(2,1)S(1)}, bf16[1,1,576,256]{3,2,0,1:T(8,128)(2,1)S(1)}, u32[]{:S(2)}, u32[]{:S(2)}) %collective-permute-start) | collective-permute-done | bytes 294944 | tf_op jit(solution)/shard_map/ppermute | solution.py:142
  321.9 17.2 %collective-permute-done.1 = bf16[1,1,576,256]{3,2,0,1:T(8,128)(2,1)S(1)} collective-permute-done((bf16[1,1,576,256]{3,2,0,1:T(8,128)(2,1)S(1)}, bf16[1,1,576,256]{3,2,0,1:T(8,128)(2,1)S(1)}, u32[]{:S(2)}, u32[]{:S(2)}) %collective-permute-start.1) | collective-permute-done | bytes 294944 | tf_op jit(solution)/shard_map/ppermute | solution.py:142
  339.9 2.4 collective-permute-done.2
  (60 shorter events, 30.6 us)
Async XLA Ops:
  6.5 129.2 %copy-start = (bf16[576,1152]{1,0:T(8,128)(2,1)S(1)}, bf16[576,1152]{1,0:T(8,128)(2,1)}, u32[]{:S(2)}) copy-start(bf16[576,1152]{1,0:T(8,128)(2,1)} %param.20) | copy-start | bytes 3981316
  6.5 39.4 %all-gather.12.cloned.1.call-start = ((), (), s32[]{:S(2)}) async-start(), calls=%async_computation.3 | async-start | bytes 3538944 | tf_op jit(solution)/shard_map/all_gather | solution.py:70
  7.3 128.5 %all-gather.8.cloned.1.call-start = ((), (), s32[]{:S(2)}) async-start(), calls=%async_computation.1 | async-start | bytes 3538944 | tf_op jit(solution)/shard_map/all_gather | solution.py:109
  45.9 2.4 copy-start.4
  99.5 131.0 %all-gather.14.cloned.1.call-start = ((), (), s32[]{:S(2)}) async-start(), calls=%async_computation.4 | async-start | bytes 3538944 | tf_op jit(solution)/shard_map/all_gather | solution.py:115
  192.0 1.8 copy-start.6
  193.5 115.0 %all-gather.10.cloned.1.call-start = ((), (), s32[]{:S(2)}) async-start(), calls=%async_computation.2 | async-start | bytes 3538944 | tf_op jit(solution)/shard_map/all_gather | solution.py:133
  230.6 2.4 copy-start.5
  257.7 2.2 copy-start.1
  268.2 40.4 %copy-start.2 = (bf16[1,576,4,256]{3,1,2,0:T(8,128)(2,1)S(1)}, bf16[1,576,4,256]{3,1,2,0:T(8,128)(2,1)}, u32[]{:S(2)}) copy-start(bf16[1,576,4,256]{3,1,2,0:T(8,128)(2,1)} %copy.46) | copy-start | bytes 3538948
  312.3 1.0 copy-start.3
  313.4 7.8 %collective-permute-start = (bf16[1,1,576,256]{3,2,0,1:T(8,128)(2,1)S(1)}, bf16[1,1,576,256]{3,2,0,1:T(8,128)(2,1)S(1)}, u32[]{:S(2)}, u32[]{:S(2)}) collective-permute-start(bf16[1,1,576,256]{3,2,0,1:T(8,128)(2,1)S(1)} %get-tuple-element.65), channel_id=1, source_target_pairs={{0,4},{4,8},{8,12},{12,0},{1,5},{5,9},{9,13},{13,1},{2,6},{6,10},{... | collective-permute-start | bytes 884744 | tf_op jit(solution)/shard_map/ppermute | solution.py:142
  314.7 24.5 %collective-permute-start.1 = (bf16[1,1,576,256]{3,2,0,1:T(8,128)(2,1)S(1)}, bf16[1,1,576,256]{3,2,0,1:T(8,128)(2,1)S(1)}, u32[]{:S(2)}, u32[]{:S(2)}) collective-permute-start(bf16[1,1,576,256]{3,2,0,1:T(8,128)(2,1)S(1)} %get-tuple-element.64), channel_id=1, source_target_pairs={{0,8},{4,12},{8,0},{12,4},{1,9},{5,13},{9,1},{13,5},{2,10},{6,14},... | collective-permute-start | bytes 884744 | tf_op jit(solution)/shard_map/ppermute | solution.py:142
  315.8 26.5 %collective-permute-start.2 = (bf16[1,1,576,256]{3,2,0,1:T(8,128)(2,1)S(1)}, bf16[1,1,576,256]{3,2,0,1:T(8,128)(2,1)S(1)}, u32[]{:S(2)}, u32[]{:S(2)}) collective-permute-start(bf16[1,1,576,256]{3,2,0,1:T(8,128)(2,1)S(1)} %get-tuple-element.63), channel_id=1, source_target_pairs={{0,12},{4,0},{8,4},{12,8},{1,13},{5,1},{9,5},{13,9},{2,14},{6,2},{... | collective-permute-start | bytes 884744 | tf_op jit(solution)/shard_map/ppermute | solution.py:142
  344.4 3.2 collective-permute-start.3
Sparse Core Ops, SparseCore 0:
  8.9 37.0 all-gather.11
  99.7 36.0 all-gather.7
  193.6 36.8 all-gather.13
  272.5 36.0 all-gather.9
